TPU v7x, 32 devices: a whole 2x2x4 slice. The times are simulated.
32 devices in a mesh: grp: 2 (over x), ep: 16 (over z, y, core).
Axes of the slice: x: 2, y: 2, z: 4, core: 2. Of those that a mesh axis runs over, the one named last changes fastest.
Arguments:
- expert_ids: int32 [2048, 8], P(('grp', 'ep')), parts along dimension 0, may hold values from 0 to 15, all different within a row; in each aligned block of 64 rows (0 to 63, 64 to 127, ...) at most 64 rows name the same one
- route_gates: float32 [2048, 8], P(('grp', 'ep')), parts along dimension 0, may hold values from 0.1 to 0.5
- routed_in: bfloat16 [2048, 8, 2048], P(('grp', 'ep')), parts along dimension 0, may hold values from -6 to 6
- down_weight: bfloat16 [16, 1024, 3584], P('ep'), may hold values from -0.1875 to 0.1875
- slot_offset: int32 [1], replicated, may hold values from 0 to 15
Outputs:
- combined: bfloat16 [2048, 3584], P(('grp', 'ep')), parts along dimension 0
There are 2 independent parts, one for each index of `grp`. A program takes and returns all parts, laid end to end along the dimension named above; an argument that names none is the same for every part. Nothing has to cross between parts.
Inputs may be any that keep to these rules, and one draw needn't show every extreme that they name: `expert_ids`: each row names 8 different experts. Among the tokens of one ep device, no expert is named by more than 64 tokens, a bound that some block reaches in some devices.
All inputs are finite; a program needn't handle non-finite values.
Results may differ from a plain program's by a relative error of at most 0.0057.
Values may be sent and summed in bfloat16 or wider, within the bound.
A program may use at most 128 MiB of HBM per device.

v0:
```python
import functools

import jax
import jax.numpy as jnp
from jax import lax
from jax.experimental import pallas as pl
from jax.experimental.pallas import tpu as pltpu
from jax.sharding import PartitionSpec as P

MESH = pl.DeviceIdType.MESH
TILE = 256
CHUNKS = 4
AHEAD = 3
VMEM_LIMIT = 63 * 1024 * 1024


def swiglu(packed):
    half = packed.shape[-1] // 2
    gate = packed[..., :half].astype(jnp.float32)
    upper = packed[..., half:].astype(jnp.float32)
    return (jax.nn.silu(gate) * upper).astype(jnp.bfloat16)


def exchange_form(expert_ids, route_gates, routed_in, down_weight, slot_offset):
    experts = lax.axis_size("ep")
    tokens_here, chosen = expert_ids.shape
    pair_count = tokens_here * chosen
    capacity = 2 * pair_count // experts
    matrix = down_weight[0]
    offset = slot_offset[0]
    target = jnp.mod(expert_ids.reshape(pair_count) - offset, experts)
    onehot = (target[:, None] == jnp.arange(experts, dtype=jnp.int32)[None, :]).astype(jnp.int32)
    earlier = jnp.cumsum(onehot, axis=0) - onehot
    rank = jnp.sum(earlier * onehot, axis=1)
    row_index = target * capacity + rank
    source = (
        jnp.full((experts * capacity,), pair_count, jnp.int32)
        .at[row_index]
        .set(jnp.arange(pair_count, dtype=jnp.int32))
    )
    payload = swiglu(routed_in.reshape(pair_count, routed_in.shape[2]))
    padded = jnp.concatenate([payload, jnp.zeros((1, payload.shape[1]), jnp.bfloat16)], axis=0)
    outgoing = jnp.take(padded, source, axis=0).reshape(experts, capacity, payload.shape[1])
    results = jnp.einsum(
        "nkf,fd->nkd",
        lax.all_to_all(outgoing, "ep", split_axis=0, concat_axis=0, tiled=True),
        matrix,
        preferred_element_type=jnp.float32,
    ).astype(jnp.bfloat16)
    returned = lax.all_to_all(results, "ep", split_axis=0, concat_axis=0, tiled=True)
    width = returned.shape[2]
    picked = jnp.take(returned.reshape(experts * capacity, width), row_index, axis=0).reshape(
        tokens_here, chosen, width
    )
    total = jnp.zeros((tokens_here, width), jnp.float32)
    for choice_index in range(chosen):
        total = total + route_gates[:, choice_index, None] * picked[:, choice_index].astype(
            jnp.float32
        )
    return total.astype(jnp.bfloat16)


def flipped(index, distance):
    result, bit = index, 1
    while bit <= distance:
        if distance & bit:
            result = result + bit - 2 * bit * lax.rem(lax.div(index, bit), 2)
        bit *= 2
    return result


def slot_distance(n, slot):
    groups = n // 4
    return (groups - 1 - slot % groups) * 4 + (slot // groups % 2) * 2 + slot // (2 * groups)


def kernel(
    n,
    target_ref,
    gate_ref,
    x_hbm,
    w_hbm,
    out_ref,
    x,
    w,
    outg,
    recv,
    own,
    psend,
    crecv,
    ysend,
    yrecv,
    zsend,
    zrecv,
    wsem,
    xsem,
    dsend_sem,
    drecv_sem,
    csend_sem,
    crecv_sem,
    ysend_sem,
    yrecv_sem,
    zsend_sem,
    zrecv_sem,
):
    me = lax.axis_index("ep")
    chosen = target_ref.shape[1]
    features, width = w.shape
    chunks, rows_all, _ = recv.shape
    part = rows_all // n
    pairs = part * chosen
    groups = n // 4
    plane = groups * part

    def send(src, dst, send_sem, recv_sem, distance):
        copy = pltpu.make_async_remote_copy(
            src_ref=src,
            dst_ref=dst,
            send_sem=send_sem,
            recv_sem=recv_sem,
            device_id={"ep": flipped(me, distance)},
            device_id_type=MESH,
        )
        copy.start()
        return copy

    barrier = pltpu.get_barrier_semaphore()
    for d in range(1, n):
        pl.semaphore_signal(barrier, inc=1, device_id={"ep": flipped(me, d)}, device_id_type=MESH)
    x_copies = []
    for k in range(chunks):
        tokens_of = pl.ds(k * part, part)
        x_copies.append(pltpu.make_async_copy(x_hbm.at[tokens_of], x.at[tokens_of], xsem.at[k]))
        x_copies[k].start()
    w_copy = pltpu.make_async_copy(w_hbm.at[0], w, wsem.at[0])
    w_copy.start()

    lane = lax.broadcasted_iota(jnp.int32, (chosen, pairs), 1)
    spread = (lane % chosen == lax.broadcasted_iota(jnp.int32, (chosen, pairs), 0)).astype(jnp.bfloat16)
    mine = (
        lax.broadcasted_iota(jnp.int32, (rows_all, pairs), 1) // chosen
        == lax.broadcasted_iota(jnp.int32, (rows_all, pairs), 0) % part
    )
    slots = [slot_distance(n, s) for s in range(n)]
    peers = [flipped(me, d) for d in slots]
    dispatch = {}

    def issue(k):
        for d in range(1, n):
            s = slots.index(d)
            here = pl.ds(s * part, part)
            dispatch[k, s] = send(
                outg.at[k, here], recv.at[k, here], dsend_sem.at[k, s], drecv_sem.at[k, s], d
            )

    for k in range(chunks):
        target = target_ref[k * part : (k + 1) * part]
        gates = gate_ref[k * part : (k + 1) * part]
        hit = jnp.concatenate([jnp.where(target == e, 1.0, 0.0) for e in peers], axis=0)
        scale = jnp.sum(hit * jnp.concatenate([gates] * n, axis=0), axis=1, keepdims=True)
        wanted = jnp.dot(hit.astype(jnp.bfloat16), spread, preferred_element_type=jnp.float32)
        pick = jnp.where(mine, wanted, 0.0).astype(jnp.bfloat16)
        x_copies[k].wait()
        for c in range(0, features, TILE):
            gate = x[k * part : (k + 1) * part, :, c : c + TILE].astype(jnp.float32)
            upper = x[k * part : (k + 1) * part, :, features + c : features + c + TILE].astype(jnp.float32)
            hidden = (jax.nn.silu(gate) * upper).reshape(pairs, TILE).astype(jnp.bfloat16)
            rows = jnp.dot(pick, hidden, preferred_element_type=jnp.float32)
            rows = (rows * scale).astype(jnp.bfloat16)
            for s, d in enumerate(slots):
                if d:
                    outg[k, s * part : (s + 1) * part, c : c + TILE] = rows[s * part : (s + 1) * part]
                else:
                    recv[k, s * part : (s + 1) * part, c : c + TILE] = rows[s * part : (s + 1) * part]
        if k == 0:
            pl.semaphore_wait(barrier, n - 1)
        if k < AHEAD:
            issue(k)
    w_copy.wait()

    core, side, line = {}, {}, {}

    def row_of(dz):
        return pl.ds((groups - 1 - dz) * part, part)

    def multiply(k):
        for s, d in enumerate(slots):
            if d:
                dispatch[k, s].wait_recv()

        @pl.loop(0, width // TILE)
        def _(j):
            here = pl.ds(pl.multiple_of(j * TILE, TILE), TILE)
            result = jnp.dot(recv[k], w[:, here], preferred_element_type=jnp.float32)
            own[k, :, here] = result[: 2 * plane]
            psend[k, :, here] = result[2 * plane :].astype(jnp.bfloat16)

        core[k] = send(psend.at[k], crecv.at[k], csend_sem.at[k], crecv_sem.at[k], 1)

    def finish_core(k):
        core[k].wait_recv()
        for p in range(2):
            here = pl.ds(p * plane // 2, plane // 2)
            there = pl.ds(plane + p * plane // 2, plane // 2)
            ysend[k, here] = (own[k, there] + crecv[k, there].astype(jnp.float32)).astype(jnp.bfloat16)
            side[k, p] = send(
                ysend.at[k, here], yrecv.at[k, here], ysend_sem.at[k, p], yrecv_sem.at[k, p], 2
            )
        own[k, 0:plane] = own[k, 0:plane] + crecv[k, 0:plane].astype(jnp.float32)

    def start_line(k, dz, bit, value):
        zsend[k, dz] = value.astype(jnp.bfloat16)
        line[k, dz] = send(
            zsend.at[k, dz], zrecv.at[k, dz], zsend_sem.at[k, dz], zrecv_sem.at[k, dz], 4 * bit
        )

    def finish_side(k):
        for p in range(2):
            side[k, p].wait_recv()
            for dz in range(groups - 1 - p * groups // 2, groups // 2 - 1 - p * groups // 2, -1):
                value = own[k, row_of(dz)] + yrecv[k, row_of(dz)].astype(jnp.float32)
                if dz % 2:
                    start_line(k, dz, 1, value)
                else:
                    own[k, row_of(dz)] = value

    def finish_line(k, bit):
        for dz in range(groups - 2 * bit, -1, -2 * bit):
            line[k, dz + bit].wait_recv()
            value = own[k, row_of(dz)] + zrecv[k, dz + bit].astype(jnp.float32)
            if dz == 0 and 2 * bit == groups:
                out_ref[k * part : (k + 1) * part] = value.astype(jnp.bfloat16)
            elif dz % (4 * bit):
                start_line(k, dz, 2 * bit, value)
            else:
                own[k, row_of(dz)] = value

    levels = groups.bit_length() - 1
    for turn in range(chunks + 1 + levels):
        if turn < chunks:
            multiply(turn)
            finish_core(turn)
            if turn + AHEAD < chunks:
                issue(turn + AHEAD)
        for level in range(levels - 1, -1, -1):
            if 0 <= turn - 2 - level < chunks:
                finish_line(turn - 2 - level, 1 << level)
        if 0 <= turn - 1 < chunks:
            finish_side(turn - 1)
    for copies in (dispatch, core, side, line):
        for copy in copies.values():
            copy.wait_send()


def scratch_of(n, tokens, chosen, features, width):
    part = tokens // CHUNKS
    plane = n // 4 * part
    small = jnp.bfloat16
    return [
        ((tokens, chosen, 2 * features), small),
        ((features, width), small),
        ((CHUNKS, n * part, features), small),
        ((CHUNKS, n * part, features), small),
        ((CHUNKS, 2 * plane, width), jnp.float32),
        ((CHUNKS, 2 * plane, width), small),
        ((CHUNKS, 2 * plane, width), small),
        ((CHUNKS, plane, width), small),
        ((CHUNKS, plane, width), small),
        ((CHUNKS, n // 4, part, width), small),
        ((CHUNKS, n // 4, part, width), small),
    ]


def bytes_of(buffers):
    total = 0
    for shape, kind in buffers:
        size = jnp.dtype(kind).itemsize
        for extent in shape:
            size *= extent
        total += size
    return total


def on_device(expert_ids, route_gates, routed_in, down_weight, slot_offset):
    n = lax.axis_size("ep")
    tokens, chosen = expert_ids.shape
    features, width = down_weight.shape[1:]
    buffers = scratch_of(n, tokens, chosen, features, width)
    if (
        n < 8
        or n & (n - 1)
        or tokens % (16 * CHUNKS)
        or chosen % 8
        or features % TILE
        or width % TILE
        or bytes_of(buffers) > VMEM_LIMIT * 3 // 4
    ):
        return exchange_form(expert_ids, route_gates, routed_in, down_weight, slot_offset)
    target = jnp.mod(expert_ids - slot_offset[0], n)
    dma = pltpu.SemaphoreType.DMA
    return pl.pallas_call(
        functools.partial(kernel, n),
        out_shape=jax.ShapeDtypeStruct((tokens, width), jnp.bfloat16),
        in_specs=[pl.BlockSpec(memory_space=pltpu.VMEM)] * 2 + [pl.BlockSpec(memory_space=pl.ANY)] * 2,
        out_specs=pl.BlockSpec(memory_space=pltpu.VMEM),
        scratch_shapes=[pltpu.VMEM(shape, kind) for shape, kind in buffers]
        + [dma((1,)), dma((CHUNKS,))]
        + [dma((CHUNKS, n))] * 2
        + [dma((CHUNKS,))] * 2
        + [dma((CHUNKS, 2))] * 2
        + [dma((CHUNKS, n // 4))] * 2,
        compiler_params=pltpu.CompilerParams(
            collective_id=0, has_side_effects=True, vmem_limit_bytes=VMEM_LIMIT
        ),
    )(target, route_gates, routed_in, down_weight)


def solution(mesh):
    placed = (
        P(("grp", "ep"), None),
        P(("grp", "ep"), None),
        P(("grp", "ep"), None, None),
        P("ep", None, None),
        P(),
    )
    return jax.shard_map(
        on_device, mesh=mesh, in_specs=placed, out_specs=P(("grp", "ep"), None), check_vma=False
    )
```

profile of v0, /device:TPU:0, one launch (start us, length us, event | category | flops | bytes accessed | tf_op | source)
XLA Modules:
  0.0 95.0 jit_solution(2034018637451555479)
XLA Ops:
  0.7 0.8 copy.6
  1.4 0.6 add_select_fusion.target_ref
  2.1 1.4 %copy.7.gate_ref = f32[64,8]{1,0:T(8,128)} copy(f32[64,8]{0,1:T(8,128)} %param.6) | data formatting | bytes 4096 | tf_op args[1]
  3.4 89.8 %shard_map.55 = bf16[64,3584]{1,0:T(8,128)(2,1)} custom-call(s32[64,8]{1,0:T(8,128)} %add_select_fusion.target_ref, f32[64,8]{1,0:T(8,128)} %copy.7.gate_ref, bf16[64,8,2048]{2,1,0:T(8,128)(2,1)} %x_hbm.1, bf16[1,1024,3584]{2,1,0:T(8,128)(2,1)} %w_hbm.1), custom_call_target="tpu_custom_call" | custom-call | tf_op jit(solution)/shard_map/pallas_call | solution.py:301
  93.2 1.8 %copy.10 = bf16[64,3584]{1,0:T(8,128)(2,1)} copy(bf16[64,3584]{1,0:T(8,128)(2,1)} %shard_map.55) | data formatting | bytes 917504
where the time goes:
time: 95.3 us; the launch traced here: 95 us
  Pallas kernels  89.8 us (94%)
  local copies, waits for them, and re-layouts  3.96 us (4%)
    pallas_call x1, Pallas kernels, on_device(): pl.pallas_call(functools.partial(kernel, n), out_shape=jax.ShapeDtypeStru...  89.8 us
    unnamed x3, local copies, waits for them, and re-layouts  3.96 us

commit v1 on v0

v1 whole, which is shorter than its diff:
```python
import functools

import jax
import jax.numpy as jnp
from jax import lax
from jax.experimental import pallas as pl
from jax.experimental.pallas import tpu as pltpu
from jax.sharding import PartitionSpec as P

MESH = pl.DeviceIdType.MESH
TILE = 256
COLUMNS = 896
PART = 8
LEAD = 2
LAG = 2
VMEM_LIMIT = 63 * 1024 * 1024


def swiglu(packed):
    half = packed.shape[-1] // 2
    gate = packed[..., :half].astype(jnp.float32)
    upper = packed[..., half:].astype(jnp.float32)
    return (jax.nn.silu(gate) * upper).astype(jnp.bfloat16)


def exchange_form(expert_ids, route_gates, routed_in, down_weight, slot_offset):
    experts = lax.axis_size("ep")
    tokens_here, chosen = expert_ids.shape
    pair_count = tokens_here * chosen
    capacity = 2 * pair_count // experts
    matrix = down_weight[0]
    offset = slot_offset[0]
    target = jnp.mod(expert_ids.reshape(pair_count) - offset, experts)
    onehot = (target[:, None] == jnp.arange(experts, dtype=jnp.int32)[None, :]).astype(jnp.int32)
    earlier = jnp.cumsum(onehot, axis=0) - onehot
    rank = jnp.sum(earlier * onehot, axis=1)
    row_index = target * capacity + rank
    source = (
        jnp.full((experts * capacity,), pair_count, jnp.int32)
        .at[row_index]
        .set(jnp.arange(pair_count, dtype=jnp.int32))
    )
    payload = swiglu(routed_in.reshape(pair_count, routed_in.shape[2]))
    padded = jnp.concatenate([payload, jnp.zeros((1, payload.shape[1]), jnp.bfloat16)], axis=0)
    outgoing = jnp.take(padded, source, axis=0).reshape(experts, capacity, payload.shape[1])
    results = jnp.einsum(
        "nkf,fd->nkd",
        lax.all_to_all(outgoing, "ep", split_axis=0, concat_axis=0, tiled=True),
        matrix,
        preferred_element_type=jnp.float32,
    ).astype(jnp.bfloat16)
    returned = lax.all_to_all(results, "ep", split_axis=0, concat_axis=0, tiled=True)
    width = returned.shape[2]
    picked = jnp.take(returned.reshape(experts * capacity, width), row_index, axis=0).reshape(
        tokens_here, chosen, width
    )
    total = jnp.zeros((tokens_here, width), jnp.float32)
    for choice_index in range(chosen):
        total = total + route_gates[:, choice_index, None] * picked[:, choice_index].astype(
            jnp.float32
        )
    return total.astype(jnp.bfloat16)


def flipped(index, distance):
    result, bit = index, 1
    while bit <= distance:
        if distance & bit:
            result = result + bit - 2 * bit * lax.rem(lax.div(index, bit), 2)
        bit *= 2
    return result


def slot_distance(n, slot):
    groups = n // 4
    return (groups - 1 - slot % groups) * 4 + (slot // groups % 2) * 2 + slot // (2 * groups)


def kernel(
    n,
    offset_ref,
    ids_ref,
    gate_ref,
    x_hbm,
    w_hbm,
    out_ref,
    x,
    w,
    outg,
    recv,
    lhs,
    own,
    psend,
    crecv,
    ysend,
    yrecv,
    zsend,
    zrecv,
    wsem,
    xsem,
    dsend_sem,
    drecv_sem,
    csend_sem,
    crecv_sem,
    ysend_sem,
    yrecv_sem,
    zsend_sem,
    zrecv_sem,
):
    me = lax.axis_index("ep")
    features, width = w.shape
    chunks, _, part, _ = recv.shape
    chosen = ids_ref.shape[0]
    pairs = part * chosen
    rows_all = n * part
    groups = n // 4
    half = n // 2
    line_at = me // 4
    at_end = jnp.logical_or(line_at == 0, line_at == groups - 1)

    def remote(src, dst, send_sem, recv_sem, distance):
        return pltpu.make_async_remote_copy(
            src_ref=src,
            dst_ref=dst,
            send_sem=send_sem,
            recv_sem=recv_sem,
            device_id={"ep": flipped(me, distance)},
            device_id_type=MESH,
        )

    def send(*args):
        copy = remote(*args)
        copy.start()
        return copy

    barrier = pltpu.get_barrier_semaphore()
    for d in range(1, n):
        pl.semaphore_signal(barrier, inc=1, device_id={"ep": flipped(me, d)}, device_id_type=MESH)
    x_copies = []
    for k in range(chunks):
        tokens_of = pl.ds(k * part, part)
        x_copies.append(pltpu.make_async_copy(x_hbm.at[tokens_of], x.at[tokens_of], xsem.at[k]))
        x_copies[k].start()
    w_copy = pltpu.make_async_copy(w_hbm.at[0], w, wsem.at[0])
    w_copy.start()

    slots = [slot_distance(n, s) for s in range(n)]
    peers = [flipped(me, d) for d in slots]
    target_all = lax.rem(ids_ref[...] - offset_ref[0] + n, n).astype(jnp.float32).T
    gates_all = gate_ref[...].T
    lane = lax.broadcasted_iota(jnp.int32, (chosen, pairs), 1)
    spread = (lane % chosen == lax.broadcasted_iota(jnp.int32, (chosen, pairs), 0)).astype(jnp.bfloat16)
    mine = (
        lax.broadcasted_iota(jnp.int32, (rows_all, pairs), 1) // chosen
        == lax.broadcasted_iota(jnp.int32, (rows_all, pairs), 0) % part
    )
    peer_of = jnp.concatenate([jnp.full((part, chosen), e, jnp.int32) for e in peers], axis=0).astype(
        jnp.float32
    )

    dispatch = {}
    for k in range(chunks):
        for s, d in enumerate(slots):
            if d:
                dispatch[k, d] = remote(
                    outg.at[k, s], recv.at[k, s], dsend_sem.at[k, s], drecv_sem.at[k, s], d
                )

    def issue(k, lines):
        if k < chunks:
            for dz in lines:
                for low in (2, 3, 0, 1):
                    if dz * 4 + low:
                        dispatch[k, dz * 4 + low].start()

    near, far = (0, 1), tuple(range(groups - 1, 1, -1))

    def issue_early(k):
        issue(k, (0,))

        @pl.when(jnp.logical_not(at_end))
        def _():
            issue(k, far + (1,))

        @pl.when(at_end)
        def _():
            if k < LEAD + 2:
                issue(k, (1,))
            if 0 < k <= LEAD:
                issue(k - 1, far)

    def issue_late(k):
        @pl.when(at_end)
        def _():
            issue(k + LEAD + 2, (1,))
            issue(k + LEAD, far)

    for k in range(chunks):
        target = target_all[k * part : (k + 1) * part]
        gates = gates_all[k * part : (k + 1) * part]
        hit = jnp.where(jnp.concatenate([target] * n, axis=0) == peer_of, 1.0, 0.0)
        scale = jnp.sum(hit * jnp.concatenate([gates] * n, axis=0), axis=1, keepdims=True)
        wanted = jnp.dot(hit.astype(jnp.bfloat16), spread, preferred_element_type=jnp.float32)
        pick = jnp.where(mine, wanted, 0.0).astype(jnp.bfloat16)
        x_copies[k].wait()
        for c in range(0, features, TILE):
            gate = x[k * part : (k + 1) * part, :, c : c + TILE].astype(jnp.float32)
            upper = x[k * part : (k + 1) * part, :, features + c : features + c + TILE].astype(jnp.float32)
            hidden = (jax.nn.silu(gate) * upper).reshape(pairs, TILE).astype(jnp.bfloat16)
            rows = jnp.dot(pick, hidden, preferred_element_type=jnp.float32)
            rows = (rows * scale).reshape(n, part, TILE).astype(jnp.bfloat16)
            for s, d in enumerate(slots):
                if d:
                    outg[k, s, :, c : c + TILE] = rows[s]
                else:
                    recv[k, s, :, c : c + TILE] = rows[s]
        if k == 0:
            pl.semaphore_wait(barrier, n - 1)
        issue_early(k)
    w_copy.wait()

    core, side, line = {}, {}, {}
    halves = 2
    span = width // halves

    def multiply(k):
        for d in slots:
            if d:
                dispatch[k, d].wait_recv()
        issue_late(k)
        lhs[...] = recv[k].astype(jnp.float32).reshape(rows_all, features).astype(jnp.bfloat16)
        for h in range(halves):

            @pl.loop(0, span // COLUMNS)
            def _(j):
                here = pl.ds(pl.multiple_of(h * span + j * COLUMNS, 128), COLUMNS)
                result = jnp.dot(lhs[...], w[:, here], preferred_element_type=jnp.float32)
                result = result.reshape(n, part, COLUMNS)
                own[k, :, :, here] = result[:half]
                psend[k, :, :, here] = result[half:].astype(jnp.bfloat16)

            cols = pl.ds(h * span, span)
            core[k, h] = send(
                psend.at[k, :, :, cols],
                crecv.at[k, :, :, cols],
                csend_sem.at[k, h],
                crecv_sem.at[k, h],
                1,
            )

    order = [dz for dz in range(groups - 1, -1, -1) if dz % 2] + [
        dz for dz in range(groups - 1, -1, -1) if dz % 2 == 0
    ]

    def summed(k, s):
        return own[k, s] + crecv[k, s].astype(jnp.float32)

    def finish_core(k):
        for h in range(halves):
            core[k, h].wait_recv()
        for dz in order:
            ysend[k, dz] = summed(k, groups + groups - 1 - dz).astype(jnp.bfloat16)
            side[k, dz] = send(
                ysend.at[k, dz], yrecv.at[k, dz], ysend_sem.at[k, dz], yrecv_sem.at[k, dz], 2
            )

    def start_line(k, dz, bit, value):
        zsend[k, dz] = value.astype(jnp.bfloat16)
        line[k, dz] = send(
            zsend.at[k, dz], zrecv.at[k, dz], zsend_sem.at[k, dz], zrecv_sem.at[k, dz], 4 * bit
        )

    def finish_side(k):
        for dz in order:
            side[k, dz].wait_recv()
            value = summed(k, groups - 1 - dz) + yrecv[k, dz].astype(jnp.float32)
            if dz % 2:
                start_line(k, dz, 1, value)
            else:
                own[k, groups - 1 - dz] = value

    def finish_line(k, bit):
        for dz in range(groups - 2 * bit, -1, -2 * bit):
            line[k, dz + bit].wait_recv()
            value = own[k, groups - 1 - dz] + zrecv[k, dz + bit].astype(jnp.float32)
            if dz == 0 and 2 * bit == groups:
                out_ref[k] = value.astype(jnp.bfloat16)
            elif dz % (4 * bit):
                start_line(k, dz, 2 * bit, value)
            else:
                own[k, groups - 1 - dz] = value

    levels = groups.bit_length() - 1

    def settle(k, stage):
        if 0 <= k < chunks:
            if stage == 0:
                finish_side(k)
            else:
                finish_line(k, 1 << (stage - 1))

    for turn in range(chunks):
        multiply(turn)
        for stage in range(levels, -1, -1):
            settle(turn - LAG - stage, stage)
        finish_core(turn)
    done = chunks - 1 - LAG
    for turn in range(chunks, chunks + LAG + levels):
        for stage in range(levels, -1, -1):
            settle(turn - LAG - stage, stage)
    for copies in (dispatch, core, side, line):
        for copy in copies.values():
            copy.wait_send()


def scratch_of(n, tokens, chosen, features, width):
    chunks = tokens // PART
    groups, half = n // 4, n // 2
    small = jnp.bfloat16
    return [
        ((tokens, chosen, 2 * features), small),
        ((features, width), small),
        ((chunks, n, PART, features), small),
        ((chunks, n, PART, features), small),
        ((n * PART, features), small),
        ((chunks, half, PART, width), jnp.float32),
        ((chunks, half, PART, width), small),
        ((chunks, half, PART, width), small),
        ((chunks, groups, PART, width), small),
        ((chunks, groups, PART, width), small),
        ((chunks, groups, PART, width), small),
        ((chunks, groups, PART, width), small),
    ]


def bytes_of(buffers):
    total = 0
    for shape, kind in buffers:
        size = jnp.dtype(kind).itemsize
        for extent in shape:
            size *= extent
        total += size
    return total


def on_device(expert_ids, route_gates, routed_in, down_weight, slot_offset):
    n = lax.axis_size("ep")
    tokens, chosen = expert_ids.shape
    features, width = down_weight.shape[1:]
    buffers = scratch_of(n, tokens, chosen, features, width)
    if (
        n < 8
        or n & (n - 1)
        or tokens % PART
        or chosen % 8
        or features % TILE
        or width % (2 * COLUMNS)
        or bytes_of(buffers) > VMEM_LIMIT * 3 // 4
    ):
        return exchange_form(expert_ids, route_gates, routed_in, down_weight, slot_offset)
    chunks, groups = tokens // PART, n // 4
    dma = pltpu.SemaphoreType.DMA
    vmem = pl.BlockSpec(memory_space=pltpu.VMEM)
    result = pl.pallas_call(
        functools.partial(kernel, n),
        out_shape=jax.ShapeDtypeStruct((chunks, PART, width), jnp.bfloat16),
        in_specs=[pl.BlockSpec(memory_space=pltpu.SMEM), vmem, vmem]
        + [pl.BlockSpec(memory_space=pl.ANY)] * 2,
        out_specs=vmem,
        scratch_shapes=[pltpu.VMEM(shape, kind) for shape, kind in buffers]
        + [dma((1,)), dma((chunks,))]
        + [dma((chunks, n))] * 2
        + [dma((chunks, 2))] * 2
        + [dma((chunks, groups))] * 4,
        compiler_params=pltpu.CompilerParams(
            collective_id=0, has_side_effects=True, vmem_limit_bytes=VMEM_LIMIT
        ),
    )(slot_offset, expert_ids.T, route_gates.T, routed_in, down_weight)
    return result.reshape(tokens, width)


def solution(mesh):
    placed = (
        P(("grp", "ep"), None),
        P(("grp", "ep"), None),
        P(("grp", "ep"), None, None),
        P("ep", None, None),
        P(),
    )
    return jax.shard_map(
        on_device, mesh=mesh, in_specs=placed, out_specs=P(("grp", "ep"), None), check_vma=False
    )
```

time: 95.3 us -> 97 us (1.018)
  Pallas kernels: 89.8 us -> 94.2 us
  local copies, waits for them, and re-layouts: 3.96 us -> 1.82 us
    pallas_call x1, Pallas kernels: 89.8 us -> 94.2 us  [on_device(): pl.pallas_call(functools.partial(kernel, n), out_shape=jax.ShapeDtypeStru...]
    unnamed x3 -> x1, local copies, waits for them, and re-layouts: 3.96 us -> 1.82 us
where the time goes in v1:
time: 97 us; the launch traced here: 96.7 us
  Pallas kernels  94.2 us (97%)
  local copies, waits for them, and re-layouts  1.82 us (2%)
    pallas_call x1, Pallas kernels, on_device(): pl.pallas_call(functools.partial(kernel, n), out_shape=jax.ShapeDtypeStru...  94.2 us

profile of v1, /device:TPU:0, one launch (start us, length us, event | category | flops | bytes accessed | tf_op | source)
XLA Modules:
  0.0 96.7 jit_solution(15627321153649010381)
XLA Ops:
  0.7 94.2 %shard_map.55 = bf16[8,8,3584]{2,1,0:T(8,128)(2,1)} custom-call(s32[1]{0:T(128)S(6)} %copy.7.offset_ref, s32[8,64]{1,0:T(8,128)} %bitcast.4, f32[8,64]{1,0:T(8,128)} %bitcast.5, bf16[64,8,2048]{2,1,0:T(8,128)(2,1)} %x_hbm.1, bf16[1,1024,3584]{2,1,0:T(8,128)(2,1)} %w_hbm.1), custom_call_target="tpu_custom_call" | custom-call | tf_op jit(solution)/shard_map/pallas_call | solution.py:364
  94.9 1.8 %copy.8 = bf16[64,3584]{1,0:T(8,128)(2,1)} copy(bf16[64,3584]{1,0:T(8,128)(2,1)} %bitcast.3) | data formatting | bytes 917504

commit v2 on v1

--- a/solution.py
+++ b/solution.py
@@ -12,7 +12,11 @@
 COLUMNS = 896
 PART = 8
 LEAD = 2
-LAG = 2
+AHEAD = 3
+FINE = 2
+FIRST, TURN = 8.0, 6.2
+Y_FIRST, Y_TURN = 21.9, 6.2
+Z_STEP, Z_FLOOR = (8.7, 8.0), 54.0
 VMEM_LIMIT = 63 * 1024 * 1024
 
 
@@ -133,6 +137,9 @@
         copy.start()
         return copy
 
+    def fine(k):
+        return k >= chunks - FINE
+
     barrier = pltpu.get_barrier_semaphore()
     for d in range(1, n):
         pl.semaphore_signal(barrier, inc=1, device_id={"ep": flipped(me, d)}, device_id_type=MESH)
@@ -159,12 +166,12 @@
     )
 
     dispatch = {}
+    others = [s for s, d in enumerate(slots) if d]
     for k in range(chunks):
-        for s, d in enumerate(slots):
-            if d:
-                dispatch[k, d] = remote(
-                    outg.at[k, s], recv.at[k, s], dsend_sem.at[k, s], drecv_sem.at[k, s], d
-                )
+        for place, s in enumerate(others):
+            dispatch[k, slots[s]] = remote(
+                outg.at[k, place], recv.at[k, s], dsend_sem.at[0], drecv_sem.at[k], slots[s]
+            )
 
     def issue(k, lines):
         if k < chunks:
@@ -180,7 +187,7 @@
 
         @pl.when(jnp.logical_not(at_end))
         def _():
-            issue(k, far + (1,))
+            issue(k, (1,) if k > AHEAD else far + (1,))
 
         @pl.when(at_end)
         def _():
@@ -190,6 +197,11 @@
                 issue(k - 1, far)
 
     def issue_late(k):
+        @pl.when(jnp.logical_not(at_end))
+        def _():
+            if k + AHEAD + 1 < chunks:
+                issue(k + AHEAD + 1, far)
+
         @pl.when(at_end)
         def _():
             issue(k + LEAD + 2, (1,))
@@ -211,7 +223,7 @@
             rows = (rows * scale).reshape(n, part, TILE).astype(jnp.bfloat16)
             for s, d in enumerate(slots):
                 if d:
-                    outg[k, s, :, c : c + TILE] = rows[s]
+                    outg[k, others.index(s), :, c : c + TILE] = rows[s]
                 else:
                     recv[k, s, :, c : c + TILE] = rows[s]
         if k == 0:
@@ -220,16 +232,17 @@
     w_copy.wait()
 
     core, side, line = {}, {}, {}
-    halves = 2
-    span = width // halves
+    sums = [dz for dz in range(groups - 1, -1, -1) if dz % 2]
+    sums += [dz for dz in range(groups - 1, -1, -1) if dz % 2 == 0]
+    place_of = {dz: place for place, dz in enumerate(sums)}
 
     def multiply(k):
-        for d in slots:
-            if d:
-                dispatch[k, d].wait_recv()
+        remote(outg.at[k], recv.at[k, pl.ds(0, n - 1)], dsend_sem.at[0], drecv_sem.at[k], 1).wait_recv()
         issue_late(k)
         lhs[...] = recv[k].astype(jnp.float32).reshape(rows_all, features).astype(jnp.bfloat16)
-        for h in range(halves):
+        parts = 2 if fine(k) else 1
+        span = width // parts
+        for h in range(parts):
 
             @pl.loop(0, span // COLUMNS)
             def _(j):
@@ -243,74 +256,89 @@
             core[k, h] = send(
                 psend.at[k, :, :, cols],
                 crecv.at[k, :, :, cols],
-                csend_sem.at[k, h],
+                csend_sem.at[0],
                 crecv_sem.at[k, h],
                 1,
             )
 
-    order = [dz for dz in range(groups - 1, -1, -1) if dz % 2] + [
-        dz for dz in range(groups - 1, -1, -1) if dz % 2 == 0
-    ]
-
     def summed(k, s):
         return own[k, s] + crecv[k, s].astype(jnp.float32)
 
+    def pieces(k, members):
+        return [[dz] for dz in members] if fine(k) else [members]
+
     def finish_core(k):
-        for h in range(halves):
+        for h in range(2 if fine(k) else 1):
             core[k, h].wait_recv()
-        for dz in order:
-            ysend[k, dz] = summed(k, groups + groups - 1 - dz).astype(jnp.bfloat16)
-            side[k, dz] = send(
-                ysend.at[k, dz], yrecv.at[k, dz], ysend_sem.at[k, dz], yrecv_sem.at[k, dz], 2
+        for piece in pieces(k, sums):
+            for dz in piece:
+                ysend[k, place_of[dz]] = summed(k, groups + groups - 1 - dz).astype(jnp.bfloat16)
+            here = pl.ds(place_of[piece[0]], len(piece))
+            side[k, piece[0]] = send(
+                ysend.at[k, here], yrecv.at[k, here], ysend_sem.at[0], yrecv_sem.at[k, place_of[piece[0]]], 2
             )
 
-    def start_line(k, dz, bit, value):
-        zsend[k, dz] = value.astype(jnp.bfloat16)
-        line[k, dz] = send(
-            zsend.at[k, dz], zrecv.at[k, dz], zsend_sem.at[k, dz], zrecv_sem.at[k, dz], 4 * bit
-        )
+    def start_line(k, bit):
+        members = [dz for dz in sums if dz % (2 * bit) == bit]
+        for piece in pieces(k, members):
+            for dz in piece:
+                if bit == 1:
+                    if (k, dz) in side:
+                        side[k, dz].wait_recv()
+                    value = summed(k, groups - 1 - dz) + yrecv[k, place_of[dz]].astype(jnp.float32)
+                else:
+                    value = add_line(k, dz, bit // 2)
+                zsend[k, place_of[dz]] = value.astype(jnp.bfloat16)
+            here = pl.ds(place_of[piece[0]], len(piece))
+            line[k, piece[0]] = send(
+                zsend.at[k, here],
+                zrecv.at[k, here],
+                zsend_sem.at[0],
+                zrecv_sem.at[k, place_of[piece[0]]],
+                4 * bit,
+            )
+
+    def add_line(k, dz, bit):
+        if (k, dz + bit) in line:
+            line[k, dz + bit].wait_recv()
+        return own[k, groups - 1 - dz] + zrecv[k, place_of[dz + bit]].astype(jnp.float32)
 
     def finish_side(k):
-        for dz in order:
-            side[k, dz].wait_recv()
-            value = summed(k, groups - 1 - dz) + yrecv[k, dz].astype(jnp.float32)
-            if dz % 2:
-                start_line(k, dz, 1, value)
-            else:
-                own[k, groups - 1 - dz] = value
+        start_line(k, 1)
+        for dz in sums:
+            if dz % 2 == 0:
+                if (k, dz) in side:
+                    side[k, dz].wait_recv()
+                own[k, groups - 1 - dz] = summed(k, groups - 1 - dz) + yrecv[k, place_of[dz]].astype(
+                    jnp.float32
+                )
 
     def finish_line(k, bit):
-        for dz in range(groups - 2 * bit, -1, -2 * bit):
-            line[k, dz + bit].wait_recv()
-            value = own[k, groups - 1 - dz] + zrecv[k, dz + bit].astype(jnp.float32)
-            if dz == 0 and 2 * bit == groups:
-                out_ref[k] = value.astype(jnp.bfloat16)
-            elif dz % (4 * bit):
-                start_line(k, dz, 2 * bit, value)
-            else:
-                own[k, groups - 1 - dz] = value
+        if 2 * bit < groups:
+            start_line(k, 2 * bit)
+        for dz in sums:
+            if dz % (4 * bit) == 0:
+                value = add_line(k, dz, bit)
+                if 2 * bit == groups:
+                    out_ref[k] = value.astype(jnp.bfloat16)
+                else:
+                    own[k, groups - 1 - dz] = value
 
     levels = groups.bit_length() - 1
 
-    def settle(k, stage):
-        if 0 <= k < chunks:
-            if stage == 0:
-                finish_side(k)
-            else:
-                finish_line(k, 1 << (stage - 1))
-
-    for turn in range(chunks):
-        multiply(turn)
-        for stage in range(levels, -1, -1):
-            settle(turn - LAG - stage, stage)
-        finish_core(turn)
-    done = chunks - 1 - LAG
-    for turn in range(chunks, chunks + LAG + levels):
-        for stage in range(levels, -1, -1):
-            settle(turn - LAG - stage, stage)
-    for copies in (dispatch, core, side, line):
-        for copy in copies.values():
-            copy.wait_send()
+    events = []
+    for k in range(chunks):
+        events.append((FIRST + TURN * k, k, multiply, ()))
+        events.append((FIRST + TURN * k + 2.5, k, finish_core, ()))
+        summed_at = Y_FIRST + Y_TURN * k
+        events.append((summed_at, k, finish_side, ()))
+        for level in range(levels):
+            summed_at = max(summed_at + Z_STEP[min(level, 1)], Z_FLOOR * level)
+            events.append((summed_at + 0.1 * k * level, k, finish_line, (1 << level,)))
+    for _, k, step, rest in sorted(events, key=lambda event: event[:2]):
+        step(k, *rest)
+    for buffer, sem in ((outg, dsend_sem), (psend, csend_sem), (ysend, ysend_sem), (zsend, zsend_sem)):
+        remote(buffer, buffer, sem.at[0], sem.at[0], 1).wait_send()
 
 
 def scratch_of(n, tokens, chosen, features, width):
@@ -320,7 +348,7 @@
     return [
         ((tokens, chosen, 2 * features), small),
         ((features, width), small),
-        ((chunks, n, PART, features), small),
+        ((chunks, n - 1, PART, features), small),
         ((chunks, n, PART, features), small),
         ((n * PART, features), small),
         ((chunks, half, PART, width), jnp.float32),
@@ -328,8 +356,8 @@
         ((chunks, half, PART, width), small),
         ((chunks, groups, PART, width), small),
         ((chunks, groups, PART, width), small),
-        ((chunks, groups, PART, width), small),
-        ((chunks, groups, PART, width), small),
+        ((chunks, groups - 1, PART, width), small),
+        ((chunks, groups - 1, PART, width), small),
     ]
 
 
@@ -369,9 +397,9 @@
         out_specs=vmem,
         scratch_shapes=[pltpu.VMEM(shape, kind) for shape, kind in buffers]
         + [dma((1,)), dma((chunks,))]
-        + [dma((chunks, n))] * 2
-        + [dma((chunks, 2))] * 2
-        + [dma((chunks, groups))] * 4,
+        + [dma((1,)), dma((chunks,))]
+        + [dma((1,)), dma((chunks, 2))]
+        + [dma((1,)), dma((chunks, groups))] * 2,
         compiler_params=pltpu.CompilerParams(
             collective_id=0, has_side_effects=True, vmem_limit_bytes=VMEM_LIMIT
         ),

time: 97 us -> 82.1 us (0.85)
  Pallas kernels: 94.2 us -> 79.4 us
    pallas_call x1, Pallas kernels: 94.2 us -> 79.4 us  [on_device(): pl.pallas_call(functools.partial(kernel, n), out_shape=jax.ShapeDtypeStru...]
where the time goes in v2:
time: 82.1 us; the launch traced here: 81.9 us
  Pallas kernels  79.4 us (97%)
  local copies, waits for them, and re-layouts  1.82 us (2%)
    pallas_call x1, Pallas kernels, on_device(): pl.pallas_call(functools.partial(kernel, n), out_shape=jax.ShapeDtypeStru...  79.4 us
    unnamed x1, local copies, waits for them, and re-layouts  1.82 us

profile of v2, /device:TPU:0, one launch (start us, length us, event | category | flops | bytes accessed | tf_op | source)
XLA Modules:
  0.0 81.9 jit_solution(6412693647841509283)
XLA Ops:
  0.7 79.4 %shard_map.55 = bf16[8,8,3584]{2,1,0:T(8,128)(2,1)} custom-call(s32[1]{0:T(128)S(6)} %copy.7.offset_ref, s32[8,64]{1,0:T(8,128)} %bitcast.4, f32[8,64]{1,0:T(8,128)} %bitcast.5, bf16[64,8,2048]{2,1,0:T(8,128)(2,1)} %x_hbm.1, bf16[1,1024,3584]{2,1,0:T(8,128)(2,1)} %w_hbm.1), custom_call_target="tpu_custom_call" | custom-call | tf_op jit(solution)/shard_map/pallas_call | solution.py:392
  80.1 1.8 %copy.8 = bf16[64,3584]{1,0:T(8,128)(2,1)} copy(bf16[64,3584]{1,0:T(8,128)(2,1)} %bitcast.3) | data formatting | bytes 917504

commit v3 on v2

v3 whole, which is shorter than its diff:
```python
import functools

import jax
import jax.numpy as jnp
from jax import lax
from jax.experimental import pallas as pl
from jax.experimental.pallas import tpu as pltpu
from jax.sharding import PartitionSpec as P

MESH = pl.DeviceIdType.MESH
TILE = 256
COLUMNS = 896
PART = 8
LEAD, AHEAD = 2, 3
FINE, DEFER = 2, 5
FIRST, TURN = 8.0, 6.2
Y_LAG, Z_LAG = 15.1, 6.5
EARLY, LATE = 54.2, 100.0
VMEM_LIMIT = 48 * 1024 * 1024


def swiglu(packed):
    half = packed.shape[-1] // 2
    gate = packed[..., :half].astype(jnp.float32)
    upper = packed[..., half:].astype(jnp.float32)
    return (jax.nn.silu(gate) * upper).astype(jnp.bfloat16)


def exchange_form(expert_ids, route_gates, routed_in, down_weight, slot_offset):
    experts = lax.axis_size("ep")
    tokens_here, chosen = expert_ids.shape
    pair_count = tokens_here * chosen
    capacity = 2 * pair_count // experts
    matrix = down_weight[0]
    offset = slot_offset[0]
    target = jnp.mod(expert_ids.reshape(pair_count) - offset, experts)
    onehot = (target[:, None] == jnp.arange(experts, dtype=jnp.int32)[None, :]).astype(jnp.int32)
    earlier = jnp.cumsum(onehot, axis=0) - onehot
    rank = jnp.sum(earlier * onehot, axis=1)
    row_index = target * capacity + rank
    source = (
        jnp.full((experts * capacity,), pair_count, jnp.int32)
        .at[row_index]
        .set(jnp.arange(pair_count, dtype=jnp.int32))
    )
    payload = swiglu(routed_in.reshape(pair_count, routed_in.shape[2]))
    padded = jnp.concatenate([payload, jnp.zeros((1, payload.shape[1]), jnp.bfloat16)], axis=0)
    outgoing = jnp.take(padded, source, axis=0).reshape(experts, capacity, payload.shape[1])
    results = jnp.einsum(
        "nkf,fd->nkd",
        lax.all_to_all(outgoing, "ep", split_axis=0, concat_axis=0, tiled=True),
        matrix,
        preferred_element_type=jnp.float32,
    ).astype(jnp.bfloat16)
    returned = lax.all_to_all(results, "ep", split_axis=0, concat_axis=0, tiled=True)
    width = returned.shape[2]
    picked = jnp.take(returned.reshape(experts * capacity, width), row_index, axis=0).reshape(
        tokens_here, chosen, width
    )
    total = jnp.zeros((tokens_here, width), jnp.float32)
    for choice_index in range(chosen):
        total = total + route_gates[:, choice_index, None] * picked[:, choice_index].astype(
            jnp.float32
        )
    return total.astype(jnp.bfloat16)


def flipped(index, distance):
    result, bit = index, 1
    while bit <= distance:
        if distance & bit:
            result = result + bit - 2 * bit * lax.rem(lax.div(index, bit), 2)
        bit *= 2
    return result


def slot_distance(n, slot):
    groups = n // 4
    return (groups - 1 - slot % groups) * 4 + (slot // groups % 2) * 2 + slot // (2 * groups)


def is_fine(k, chunks):
    return k >= chunks - FINE


def core_parts(k, chunks):
    return 2 if is_fine(k, chunks) else 1


def side_pieces(k, chunks, groups):
    sums = list(range(groups - 1, -1, -1))
    if is_fine(k, chunks):
        return [[dz] for dz in sums]
    return [sums[:-1], sums[-1:]] if k >= chunks - DEFER else [sums]


def semaphore_plan(chunks, groups):
    keys = ["w", "ids", "gates", "x_first", "x_rest", "dispatch_out", "core_out", "side_out", "line_out"]
    for k in range(chunks):
        keys.append(("dispatch", k))
        keys += [("core", k, h) for h in range(core_parts(k, chunks))]
        keys += [("side", k, piece[0]) for piece in side_pieces(k, chunks, groups)]
        keys += [("pair", k), ("next", k), ("last", k)]
    return {key: place for place, key in enumerate(keys)}


def kernel(
    n,
    offset_ref,
    ids_hbm,
    gate_hbm,
    x_hbm,
    w_hbm,
    out_ref,
    ids,
    gates,
    x,
    w,
    outg,
    recv,
    lhs,
    own,
    psend,
    crecv,
    ysend,
    yrecv,
    zsend,
    zrecv,
    zlast,
    sems,
    ready,
):
    me = lax.axis_index("ep")
    features, width = w.shape
    chunks, _, part, _ = recv.shape
    chosen = ids.shape[0]
    pairs = part * chosen
    rows_all = n * part
    groups = n // 4
    half = n // 2
    line_at = me // 4
    at_end = jnp.logical_or(line_at == 0, line_at == groups - 1)
    inside = jnp.logical_not(at_end)
    plan = semaphore_plan(chunks, groups)

    def sem(*key):
        return sems.at[plan[key if len(key) > 1 else key[0]]]

    def remote(src, dst, send_sem, recv_sem, distance):
        return pltpu.make_async_remote_copy(
            src_ref=src,
            dst_ref=dst,
            send_sem=send_sem,
            recv_sem=recv_sem,
            device_id={"ep": flipped(me, distance)},
            device_id_type=MESH,
        )

    def local(src, dst, key):
        copy = pltpu.make_async_copy(src, dst, sem(key))
        copy.start()
        return copy

    def tell(semaphore, distance):
        pl.semaphore_signal(
            semaphore, inc=1, device_id={"ep": flipped(me, distance)}, device_id_type=MESH
        )

    barrier = pltpu.get_barrier_semaphore()
    for d in range(1, 8):
        tell(barrier, d)

    @pl.when(inside)
    def _():
        for d in range(12, 16):
            tell(barrier, d)

    ids_copy = local(ids_hbm, ids, "ids")
    gates_copy = local(gate_hbm, gates, "gates")
    first, later = pl.ds(0, part), pl.ds(part, (chunks - 1) * part)
    x_first = local(x_hbm.at[first], x.at[first], "x_first")
    x_rest = local(x_hbm.at[later], x.at[later], "x_rest")
    w_copy = local(w_hbm.at[0], w, "w")

    slots = [slot_distance(n, s) for s in range(n)]
    others = [s for s, d in enumerate(slots) if d]
    peers = [flipped(me, d) for d in slots]
    lane = lax.broadcasted_iota(jnp.int32, (chosen, pairs), 1)
    spread = (lane % chosen == lax.broadcasted_iota(jnp.int32, (chosen, pairs), 0)).astype(jnp.bfloat16)
    mine = (
        lax.broadcasted_iota(jnp.int32, (rows_all, pairs), 1) // chosen
        == lax.broadcasted_iota(jnp.int32, (rows_all, pairs), 0) % part
    )
    peer_of = jnp.concatenate([jnp.full((part, chosen), e, jnp.int32) for e in peers], axis=0).astype(
        jnp.float32
    )

    dispatch = {}
    for k in range(chunks):
        for place, s in enumerate(others):
            dispatch[k, slots[s]] = remote(
                outg.at[k, place], recv.at[k, s], sem("dispatch_out"), sem("dispatch", k), slots[s]
            )

    def issue(k, lines):
        if k < chunks:
            for dz in lines:
                for low in (2, 3, 0, 1):
                    if dz * 4 + low:
                        dispatch[k, dz * 4 + low].start()

    far = tuple(range(groups - 1, 1, -1))

    def issue_early(k):
        issue(k, (0,))

        @pl.when(inside)
        def _():
            if k == 0:
                issue(0, (3, 1))
                tell(ready, 4)
                tell(ready, 12)
            elif k == 1:
                pl.semaphore_wait(ready, 1)
                tell(ready, 4)
                issue(0, (2,))
                issue(1, far + (1,))
            else:
                issue(k, (1,) if k > AHEAD else far + (1,))

        @pl.when(at_end)
        def _():
            if k == 1:
                pl.semaphore_wait(ready, 2)
            if 0 < k <= LEAD:
                issue(k - 1, far)
            if k < LEAD + 2:
                issue(k, (1,))

    def issue_late(k):
        @pl.when(inside)
        def _():
            if k + AHEAD + 1 < chunks:
                issue(k + AHEAD + 1, far)

        @pl.when(at_end)
        def _():
            issue(k + LEAD + 2, (1,))
            issue(k + LEAD, far)

    ids_copy.wait()
    gates_copy.wait()
    target_all = lax.rem(ids[...] - offset_ref[0] + n, n).astype(jnp.float32).T
    gates_all = gates[...].T

    def prepare(k):
        target = target_all[k * part : (k + 1) * part]
        weight = gates_all[k * part : (k + 1) * part]
        hit = jnp.where(jnp.concatenate([target] * n, axis=0) == peer_of, 1.0, 0.0)
        scale = jnp.sum(hit * jnp.concatenate([weight] * n, axis=0), axis=1, keepdims=True)
        wanted = jnp.dot(hit.astype(jnp.bfloat16), spread, preferred_element_type=jnp.float32)
        pick = jnp.where(mine, wanted, 0.0).astype(jnp.bfloat16)
        if k == 0:
            x_first.wait()
        if k == 1:
            x_rest.wait()
        for c in range(0, features, TILE):
            gate = x[k * part : (k + 1) * part, :, c : c + TILE].astype(jnp.float32)
            upper = x[k * part : (k + 1) * part, :, features + c : features + c + TILE].astype(jnp.float32)
            hidden = (jax.nn.silu(gate) * upper).reshape(pairs, TILE).astype(jnp.bfloat16)
            rows = jnp.dot(pick, hidden, preferred_element_type=jnp.float32)
            rows = (rows * scale).reshape(n, part, TILE).astype(jnp.bfloat16)
            for s, d in enumerate(slots):
                if d:
                    outg[k, others.index(s), :, c : c + TILE] = rows[s]
                else:
                    recv[k, s, :, c : c + TILE] = rows[s]

    for k in range(chunks):
        prepare(k)
        if k == 0:
            pl.semaphore_wait(barrier, jnp.where(at_end, 7, 11))
        issue_early(k)
    w_copy.wait()

    core, side = {}, {}

    def multiply(k):
        remote(
            outg.at[k], recv.at[k, pl.ds(0, n - 1)], sem("dispatch_out"), sem("dispatch", k), 1
        ).wait_recv()
        issue_late(k)
        lhs[...] = recv[k].astype(jnp.float32).reshape(rows_all, features).astype(jnp.bfloat16)
        parts = core_parts(k, chunks)
        span = width // parts
        for h in range(parts):

            @pl.loop(0, span // COLUMNS)
            def _(j):
                here = pl.ds(pl.multiple_of(h * span + j * COLUMNS, 128), COLUMNS)
                result = jnp.dot(lhs[...], w[:, here], preferred_element_type=jnp.float32)
                result = result.reshape(n, part, COLUMNS)
                own[k, :, :, here] = result[:half]
                psend[k, :, :, here] = result[half:].astype(jnp.bfloat16)

            cols = pl.ds(h * span, span)
            core[k, h] = remote(
                psend.at[k, :, :, cols], crecv.at[k, :, :, cols], sem("core_out"), sem("core", k, h), 1
            )
            core[k, h].start()

    def summed(k, s):
        return own[k, s] + crecv[k, s].astype(jnp.float32)

    def at_dz(dz):
        return groups - 1 - dz

    def send_side(k, piece):
        here = pl.ds(at_dz(piece[0]), len(piece))
        side[k, piece[0]] = remote(
            ysend.at[k, here], yrecv.at[k, here], sem("side_out"), sem("side", k, piece[0]), 2
        )
        side[k, piece[0]].start()

    def finish_core(k):
        for h in range(core_parts(k, chunks)):
            core[k, h].wait_recv()
        for piece in side_pieces(k, chunks, groups):
            for dz in piece:
                ysend[k, at_dz(dz)] = summed(k, groups + at_dz(dz)).astype(jnp.bfloat16)
            if piece != [0]:
                send_side(k, piece)

    def finish_core_later(k):
        if [0] in side_pieces(k, chunks, groups):
            send_side(k, [0])

    def need_side(k, members):
        for piece in side_pieces(k, chunks, groups):
            if (k, piece[0]) in side and set(piece) & set(members):
                side.pop((k, piece[0])).wait_recv()

    def value_of(k, dz):
        return summed(k, at_dz(dz)) + yrecv[k, at_dz(dz)].astype(jnp.float32)

    def line_copy(kind, k, here, landing, distance):
        return remote(zsend.at[k, here], landing, sem("line_out"), sem(kind, k), distance)

    two, one = pl.ds(0, 2), pl.ds(2, 1)

    def start_line(k):
        need_side(k, (3, 2))

        @pl.when(at_end)
        def _():
            for dz in (3, 2):
                zsend[k, at_dz(dz)] = value_of(k, dz).astype(jnp.bfloat16)
            line_copy("pair", k, two, zrecv.at[k, two], 4).start()

        need_side(k, (1,))
        zsend[k, at_dz(1)] = value_of(k, 1).astype(jnp.bfloat16)
        line_copy("next", k, one, zrecv.at[k, one], 4).start()

    def pass_line(k):
        @pl.when(inside)
        def _():
            line_copy("pair", k, two, zrecv.at[k, two], 4).wait_recv()
            for dz, distance in ((2, 8), (3, 12)):
                added = zrecv[k, at_dz(5 - dz)].astype(jnp.float32)
                zsend[k, at_dz(dz)] = (value_of(k, dz) + added).astype(jnp.bfloat16)
                line_copy("last", k, pl.ds(at_dz(dz), 1), zlast.at[pl.ds(k, 1)], distance).start()

    def finish(k):
        need_side(k, (0,))
        line_copy("next", k, one, zrecv.at[k, one], 4).wait_recv()
        value = value_of(k, 0) + zrecv[k, at_dz(1)].astype(jnp.float32)
        line_copy("last", k, one, zlast.at[pl.ds(k, 1)], 4).wait_recv()
        out_ref[k] = (value + zlast[k].astype(jnp.float32)).astype(jnp.bfloat16)

    events = []
    for k in range(chunks):
        at = FIRST + TURN * k
        events.append((at, k, multiply))
        events.append((at + 2.5, k, finish_core))
        events.append((FIRST + TURN * (chunks - 1) + 2.55, k, finish_core_later))
        events.append((at + Y_LAG, k, start_line))
        events.append((at + Y_LAG + Z_LAG, k, pass_line))
        events.append((EARLY if k < chunks - DEFER else LATE, k, finish))
    for _, k, step in sorted(events, key=lambda event: event[:2]):
        step(k)
    for buffer, key in (
        (outg, "dispatch_out"),
        (psend, "core_out"),
        (ysend, "side_out"),
        (zsend, "line_out"),
    ):
        remote(buffer, buffer, sem(key), sem(key), 1).wait_send()


def scratch_of(n, tokens, chosen, features, width):
    chunks = tokens // PART
    groups, half = n // 4, n // 2
    small = jnp.bfloat16
    return [
        ((chosen, tokens), jnp.int32),
        ((chosen, tokens), jnp.float32),
        ((tokens, chosen, 2 * features), small),
        ((features, width), small),
        ((chunks, n - 1, PART, features), small),
        ((chunks, n, PART, features), small),
        ((n * PART, features), small),
        ((chunks, half, PART, width), jnp.float32),
        ((chunks, half, PART, width), small),
        ((chunks, half, PART, width), small),
        ((chunks, groups, PART, width), small),
        ((chunks, groups, PART, width), small),
        ((chunks, groups - 1, PART, width), small),
        ((chunks, groups - 1, PART, width), small),
        ((chunks, PART, width), small),
    ]


def bytes_of(buffers):
    total = 0
    for shape, kind in buffers:
        size = jnp.dtype(kind).itemsize
        for extent in shape:
            size *= extent
        total += size
    return total


def on_device(expert_ids, route_gates, routed_in, down_weight, slot_offset):
    n = lax.axis_size("ep")
    tokens, chosen = expert_ids.shape
    features, width = down_weight.shape[1:]
    buffers = scratch_of(n, tokens, chosen, features, width)
    if (
        n != 16
        or tokens % PART
        or tokens < 4 * PART
        or chosen % 8
        or features % TILE
        or width % (2 * COLUMNS)
        or bytes_of(buffers) > VMEM_LIMIT * 7 // 8
    ):
        return exchange_form(expert_ids, route_gates, routed_in, down_weight, slot_offset)
    chunks, groups = tokens // PART, n // 4
    in_hbm = [
        pltpu.with_memory_space_constraint(array, pltpu.HBM)
        for array in (expert_ids.T, route_gates.T, routed_in, down_weight)
    ]
    result = pl.pallas_call(
        functools.partial(kernel, n),
        out_shape=jax.ShapeDtypeStruct((chunks, PART, width), jnp.bfloat16),
        in_specs=[pl.BlockSpec(memory_space=pltpu.SMEM)] + [pl.BlockSpec(memory_space=pltpu.HBM)] * 4,
        out_specs=pl.BlockSpec(memory_space=pltpu.VMEM),
        scratch_shapes=[pltpu.VMEM(shape, kind) for shape, kind in buffers]
        + [pltpu.SemaphoreType.DMA((len(semaphore_plan(chunks, groups)),)), pltpu.SemaphoreType.REGULAR],
        compiler_params=pltpu.CompilerParams(
            collective_id=0, has_side_effects=True, vmem_limit_bytes=VMEM_LIMIT
        ),
    )(slot_offset, *in_hbm)
    return result.reshape(tokens, width)


def solution(mesh):
    placed = (
        P(("grp", "ep"), None),
        P(("grp", "ep"), None),
        P(("grp", "ep"), None, None),
        P("ep", None, None),
        P(),
    )
    return jax.shard_map(
        on_device, mesh=mesh, in_specs=placed, out_specs=P(("grp", "ep"), None), check_vma=False
    )
```

time: 82.1 us -> 75.5 us (0.920)
  Pallas kernels: 79.4 us -> 73.9 us
  local copies, waits for them, and re-layouts: 1.82 us -> 0.77 us
    pallas_call x1, Pallas kernels: 79.4 us -> 73.9 us  [on_device(): pl.pallas_call(functools.partial(kernel, n), out_shape=jax.ShapeDtypeStru...]
    unnamed x1, local copies, waits for them, and re-layouts: 1.82 us -> 0.77 us
where the time goes in v3:
time: 75.5 us; the launch traced here: 75.3 us
  Pallas kernels  73.9 us (98%)
  local copies, waits for them, and re-layouts  0.77 us (1%)
    pallas_call x1, Pallas kernels, on_device(): pl.pallas_call(functools.partial(kernel, n), out_shape=jax.ShapeDtypeStru...  73.9 us

profile of v3, /device:TPU:0, one launch (start us, length us, event | category | flops | bytes accessed | tf_op | source)
XLA Modules:
  0.0 75.3 jit_solution(1861067906247821777)
XLA Ops:
  0.7 73.9 %shard_map.55 = bf16[8,8,3584]{2,1,0:T(8,128)(2,1)S(1)} custom-call(s32[1]{0:T(128)S(6)} %copy.7.offset_ref, s32[8,64]{1,0:T(8,128)} %bitcast.4, f32[8,64]{1,0:T(8,128)} %bitcast.5, bf16[64,8,2048]{2,1,0:T(8,128)(2,1)} %x_hbm.1, bf16[1,1024,3584]{2,1,0:T(8,128)(2,1)} %w_hbm.1), custom_call_target="tpu_custom_call" | custom-call | tf_op jit(solution)/shard_map/pallas_call | solution.py:453
  74.6 0.8 %copy.8 = bf16[64,3584]{1,0:T(8,128)(2,1)} copy(bf16[64,3584]{1,0:T(8,128)(2,1)S(1)} %bitcast.3) | data formatting | bytes 917504

commit v4 on v3

--- a/solution.py
+++ b/solution.py
@@ -11,8 +11,8 @@
 TILE = 256
 COLUMNS = 896
 PART = 8
-LEAD, AHEAD = 2, 3
-FINE, DEFER = 2, 5
+LEAD, AHEAD = 3, 3
+FINE, DEFER, HOLD = 2, 5, 4
 FIRST, TURN = 8.0, 6.2
 Y_LAG, Z_LAG = 15.1, 6.5
 EARLY, LATE = 54.2, 100.0
@@ -359,7 +359,15 @@
 
         need_side(k, (1,))
         zsend[k, at_dz(1)] = value_of(k, 1).astype(jnp.bfloat16)
-        line_copy("next", k, one, zrecv.at[k, one], 4).start()
+
+        @pl.when(jnp.logical_or(inside, k < chunks - HOLD))
+        def _():
+            line_copy("next", k, one, zrecv.at[k, one], 4).start()
+
+    def send_held(k):
+        @pl.when(at_end)
+        def _():
+            line_copy("next", k, one, zrecv.at[k, one], 4).start()
 
     def pass_line(k):
         @pl.when(inside)
@@ -378,12 +386,15 @@
         out_ref[k] = (value + zlast[k].astype(jnp.float32)).astype(jnp.bfloat16)
 
     events = []
+    last_at = FIRST + TURN * (chunks - 1)
     for k in range(chunks):
         at = FIRST + TURN * k
         events.append((at, k, multiply))
         events.append((at + 2.5, k, finish_core))
-        events.append((FIRST + TURN * (chunks - 1) + 2.55, k, finish_core_later))
+        events.append((last_at + 2.55, k, finish_core_later))
         events.append((at + Y_LAG, k, start_line))
+        if k >= chunks - HOLD:
+            events.append((last_at + Y_LAG + 0.01, k, send_held))
         events.append((at + Y_LAG + Z_LAG, k, pass_line))
         events.append((EARLY if k < chunks - DEFER else LATE, k, finish))
     for _, k, step in sorted(events, key=lambda event: event[:2]):

time: 75.5 us -> 73.8 us (0.977)
  Pallas kernels: 73.9 us -> 72.2 us
    pallas_call x1, Pallas kernels: 73.9 us -> 72.2 us  [on_device(): pl.pallas_call(functools.partial(kernel, n), out_shape=jax.ShapeDtypeStru...]
where the time goes in v4:
time: 73.8 us; the launch traced here: 73.7 us
  Pallas kernels  72.2 us (98%)
  local copies, waits for them, and re-layouts  0.77 us (1%)
    pallas_call x1, Pallas kernels, on_device(): pl.pallas_call(functools.partial(kernel, n), out_shape=jax.ShapeDtypeStru...  72.2 us

profile of v4, /device:TPU:0, one launch (start us, length us, event | category | flops | bytes accessed | tf_op | source)
XLA Modules:
  0.0 73.7 jit_solution(5986564531175697183)
XLA Ops:
  0.7 72.2 %shard_map.55 = bf16[8,8,3584]{2,1,0:T(8,128)(2,1)S(1)} custom-call(s32[1]{0:T(128)S(6)} %copy.7.offset_ref, s32[8,64]{1,0:T(8,128)} %bitcast.4, f32[8,64]{1,0:T(8,128)} %bitcast.5, bf16[64,8,2048]{2,1,0:T(8,128)(2,1)} %x_hbm.1, bf16[1,1024,3584]{2,1,0:T(8,128)(2,1)} %w_hbm.1), custom_call_target="tpu_custom_call" | custom-call | tf_op jit(solution)/shard_map/pallas_call | solution.py:464
  72.9 0.8 %copy.8 = bf16[64,3584]{1,0:T(8,128)(2,1)} copy(bf16[64,3584]{1,0:T(8,128)(2,1)S(1)} %bitcast.3) | data formatting | bytes 917504

commit v5 on v4

--- a/solution.py
+++ b/solution.py
@@ -94,13 +94,18 @@
     return [sums[:-1], sums[-1:]] if k >= chunks - DEFER else [sums]
 
 
+def pair_pieces(k, chunks):
+    return [[3], [2]] if is_fine(k, chunks) else [[3, 2]]
+
+
 def semaphore_plan(chunks, groups):
     keys = ["w", "ids", "gates", "x_first", "x_rest", "dispatch_out", "core_out", "side_out", "line_out"]
     for k in range(chunks):
         keys.append(("dispatch", k))
         keys += [("core", k, h) for h in range(core_parts(k, chunks))]
         keys += [("side", k, piece[0]) for piece in side_pieces(k, chunks, groups)]
-        keys += [("pair", k), ("next", k), ("last", k)]
+        keys += [("pair", k, piece[0]) for piece in pair_pieces(k, chunks)]
+        keys += [("next", k), ("last", k)]
     return {key: place for place, key in enumerate(keys)}
 
 
@@ -128,6 +133,7 @@
     zrecv,
     zlast,
     sems,
+    side_ready,
     ready,
 ):
     me = lax.axis_index("ep")
@@ -167,12 +173,12 @@
         )
 
     barrier = pltpu.get_barrier_semaphore()
-    for d in range(1, 8):
+    for d in range(1, 6):
         tell(barrier, d)
 
     @pl.when(inside)
     def _():
-        for d in range(12, 16):
+        for d in (6, 7, 12, 13):
             tell(barrier, d)
 
     ids_copy = local(ids_hbm, ids, "ids")
@@ -202,10 +208,12 @@
                 outg.at[k, place], recv.at[k, s], sem("dispatch_out"), sem("dispatch", k), slots[s]
             )
 
-    def issue(k, lines):
+    straight, turning = (0, 1), (2, 3)
+
+    def issue(k, lines, lows=turning + straight):
         if k < chunks:
             for dz in lines:
-                for low in (2, 3, 0, 1):
+                for low in lows:
                     if dz * 4 + low:
                         dispatch[k, dz * 4 + low].start()
 
@@ -217,14 +225,19 @@
         @pl.when(inside)
         def _():
             if k == 0:
-                issue(0, (3, 1))
+                tell(side_ready, 2)
+                issue(0, (3, 1), straight)
+            elif k == 1:
+                issue(1, (3,), straight)
+                pl.semaphore_wait(side_ready, 1)
                 tell(ready, 4)
                 tell(ready, 12)
-            elif k == 1:
+                issue(0, (3, 1), turning)
                 pl.semaphore_wait(ready, 1)
                 tell(ready, 4)
                 issue(0, (2,))
-                issue(1, far + (1,))
+                issue(1, (3,), turning)
+                issue(1, (2, 1))
             else:
                 issue(k, (1,) if k > AHEAD else far + (1,))
 
@@ -279,7 +292,7 @@
     for k in range(chunks):
         prepare(k)
         if k == 0:
-            pl.semaphore_wait(barrier, jnp.where(at_end, 7, 11))
+            pl.semaphore_wait(barrier, 7)
         issue_early(k)
     w_copy.wait()
 
@@ -346,16 +359,21 @@
     def line_copy(kind, k, here, landing, distance):
         return remote(zsend.at[k, here], landing, sem("line_out"), sem(kind, k), distance)
 
-    two, one = pl.ds(0, 2), pl.ds(2, 1)
+    def pair_copy(k, piece):
+        here = pl.ds(at_dz(piece[0]), len(piece))
+        return remote(zsend.at[k, here], zrecv.at[k, here], sem("line_out"), sem("pair", k, piece[0]), 4)
+
+    one = pl.ds(2, 1)
 
     def start_line(k):
-        need_side(k, (3, 2))
-
-        @pl.when(at_end)
-        def _():
-            for dz in (3, 2):
-                zsend[k, at_dz(dz)] = value_of(k, dz).astype(jnp.bfloat16)
-            line_copy("pair", k, two, zrecv.at[k, two], 4).start()
+        for piece in pair_pieces(k, chunks):
+            need_side(k, piece)
+
+            @pl.when(at_end)
+            def _():
+                for dz in piece:
+                    zsend[k, at_dz(dz)] = value_of(k, dz).astype(jnp.bfloat16)
+                pair_copy(k, piece).start()
 
         need_side(k, (1,))
         zsend[k, at_dz(1)] = value_of(k, 1).astype(jnp.bfloat16)
@@ -372,11 +390,14 @@
     def pass_line(k):
         @pl.when(inside)
         def _():
-            line_copy("pair", k, two, zrecv.at[k, two], 4).wait_recv()
-            for dz, distance in ((2, 8), (3, 12)):
-                added = zrecv[k, at_dz(5 - dz)].astype(jnp.float32)
-                zsend[k, at_dz(dz)] = (value_of(k, dz) + added).astype(jnp.bfloat16)
-                line_copy("last", k, pl.ds(at_dz(dz), 1), zlast.at[pl.ds(k, 1)], distance).start()
+            for piece in pair_pieces(k, chunks):
+                pair_copy(k, piece).wait_recv()
+                for landed in piece:
+                    dz = 5 - landed
+                    added = zrecv[k, at_dz(landed)].astype(jnp.float32)
+                    zsend[k, at_dz(dz)] = (value_of(k, dz) + added).astype(jnp.bfloat16)
+                    here = pl.ds(at_dz(dz), 1)
+                    line_copy("last", k, here, zlast.at[pl.ds(k, 1)], 4 * dz).start()
 
     def finish(k):
         need_side(k, (0,))
@@ -467,7 +488,7 @@
         in_specs=[pl.BlockSpec(memory_space=pltpu.SMEM)] + [pl.BlockSpec(memory_space=pltpu.HBM)] * 4,
         out_specs=pl.BlockSpec(memory_space=pltpu.VMEM),
         scratch_shapes=[pltpu.VMEM(shape, kind) for shape, kind in buffers]
-        + [pltpu.SemaphoreType.DMA((len(semaphore_plan(chunks, groups)),)), pltpu.SemaphoreType.REGULAR],
+        + [pltpu.SemaphoreType.DMA((len(semaphore_plan(chunks, groups)),)), pltpu.SemaphoreType.REGULAR, pltpu.SemaphoreType.REGULAR],
         compiler_params=pltpu.CompilerParams(
             collective_id=0, has_side_effects=True, vmem_limit_bytes=VMEM_LIMIT
         ),

time: 73.8 us -> 73 us (0.989)
  Pallas kernels: 72.2 us -> 71.4 us
    pallas_call x1, Pallas kernels: 72.2 us -> 71.4 us  [on_device(): pl.pallas_call(functools.partial(kernel, n), out_shape=jax.ShapeDtypeStru...]
where the time goes in v5:
time: 73 us; the launch traced here: 72.8 us
  Pallas kernels  71.4 us (98%)
  local copies, waits for them, and re-layouts  0.77 us (1%)
    pallas_call x1, Pallas kernels, on_device(): pl.pallas_call(functools.partial(kernel, n), out_shape=jax.ShapeDtypeStru...  71.4 us

profile of v5, /device:TPU:0, one launch (start us, length us, event | category | flops | bytes accessed | tf_op | source)
XLA Modules:
  0.0 72.8 jit_solution(2887203391081713639)
XLA Ops:
  0.7 71.4 %shard_map.55 = bf16[8,8,3584]{2,1,0:T(8,128)(2,1)S(1)} custom-call(s32[1]{0:T(128)S(6)} %copy.7.offset_ref, s32[8,64]{1,0:T(8,128)} %bitcast.4, f32[8,64]{1,0:T(8,128)} %bitcast.5, bf16[64,8,2048]{2,1,0:T(8,128)(2,1)} %x_hbm.1, bf16[1,1024,3584]{2,1,0:T(8,128)(2,1)} %w_hbm.1), custom_call_target="tpu_custom_call" | custom-call | tf_op jit(solution)/shard_map/pallas_call | solution.py:485
  72.0 0.8 %copy.8 = bf16[64,3584]{1,0:T(8,128)(2,1)} copy(bf16[64,3584]{1,0:T(8,128)(2,1)S(1)} %bitcast.3) | data formatting | bytes 917504

commit v6 on v5

--- a/solution.py
+++ b/solution.py
@@ -9,12 +9,13 @@
 
 MESH = pl.DeviceIdType.MESH
 TILE = 256
-COLUMNS = 896
+COLUMNS = 1792
 PART = 8
 LEAD, AHEAD = 3, 3
 FINE, DEFER, HOLD = 2, 5, 4
 FIRST, TURN = 8.0, 6.2
 Y_LAG, Z_LAG = 15.1, 6.5
+SKIP = 2
 EARLY, LATE = 54.2, 100.0
 VMEM_LIMIT = 48 * 1024 * 1024
 
@@ -365,6 +366,10 @@
 
     one = pl.ds(2, 1)
 
+    def pass_copy(k, dz):
+        return line_copy("last", k, pl.ds(at_dz(dz), 1), zlast.at[pl.ds(k, 1)], 4 * dz)
+
+
     def start_line(k):
         for piece in pair_pieces(k, chunks):
             need_side(k, piece)
@@ -396,8 +401,13 @@
                     dz = 5 - landed
                     added = zrecv[k, at_dz(landed)].astype(jnp.float32)
                     zsend[k, at_dz(dz)] = (value_of(k, dz) + added).astype(jnp.bfloat16)
-                    here = pl.ds(at_dz(dz), 1)
-                    line_copy("last", k, here, zlast.at[pl.ds(k, 1)], 4 * dz).start()
+                    if dz == 2 or k < chunks - SKIP:
+                        pass_copy(k, dz).start()
+
+    def pass_held(k):
+        @pl.when(inside)
+        def _():
+            pass_copy(k, 3).start()
 
     def finish(k):
         need_side(k, (0,))
@@ -417,6 +427,8 @@
         if k >= chunks - HOLD:
             events.append((last_at + Y_LAG + 0.01, k, send_held))
         events.append((at + Y_LAG + Z_LAG, k, pass_line))
+        if k >= chunks - SKIP:
+            events.append((last_at + Y_LAG + Z_LAG + 0.01, k, pass_held))
         events.append((EARLY if k < chunks - DEFER else LATE, k, finish))
     for _, k, step in sorted(events, key=lambda event: event[:2]):
         step(k)

time: 73 us -> 72 us (0.986)
  Pallas kernels: 71.4 us -> 70.4 us
    pallas_call x1, Pallas kernels: 71.4 us -> 70.4 us  [on_device(): pl.pallas_call(functools.partial(kernel, n), out_shape=jax.ShapeDtypeStru...]
where the time goes in v6:
time: 72 us; the launch traced here: 71.9 us
  Pallas kernels  70.4 us (98%)
  local copies, waits for them, and re-layouts  0.77 us (1%)
    pallas_call x1, Pallas kernels, on_device(): pl.pallas_call(functools.partial(kernel, n), out_shape=jax.ShapeDtypeStru...  70.4 us

profile of v6, /device:TPU:0, one launch (start us, length us, event | category | flops | bytes accessed | tf_op | source)
XLA Modules:
  0.0 71.9 jit_solution(2311420113522308116)
XLA Ops:
  0.7 70.4 %shard_map.55 = bf16[8,8,3584]{2,1,0:T(8,128)(2,1)S(1)} custom-call(s32[1]{0:T(128)S(6)} %copy.7.offset_ref, s32[8,64]{1,0:T(8,128)} %bitcast.4, f32[8,64]{1,0:T(8,128)} %bitcast.5, bf16[64,8,2048]{2,1,0:T(8,128)(2,1)} %x_hbm.1, bf16[1,1024,3584]{2,1,0:T(8,128)(2,1)} %w_hbm.1), custom_call_target="tpu_custom_call" | custom-call | tf_op jit(solution)/shard_map/pallas_call | solution.py:497
  71.1 0.8 %copy.8 = bf16[64,3584]{1,0:T(8,128)(2,1)} copy(bf16[64,3584]{1,0:T(8,128)(2,1)S(1)} %bitcast.3) | data formatting | bytes 917504

commit v7 on v6

--- a/solution.py
+++ b/solution.py
@@ -218,7 +218,7 @@
                     if dz * 4 + low:
                         dispatch[k, dz * 4 + low].start()
 
-    far = tuple(range(groups - 1, 1, -1))
+    far = tuple(range(2, groups))
 
     def issue_early(k):
         issue(k, (0,))

time: 72 us -> 72 us (level)
  no operation moved by 1% of the time
where the time goes in v7:
time: 72 us; the launch traced here: 71.8 us
  Pallas kernels  70.4 us (98%)
  local copies, waits for them, and re-layouts  0.77 us (1%)
    pallas_call x1, Pallas kernels, on_device(): pl.pallas_call(functools.partial(kernel, n), out_shape=jax.ShapeDtypeStru...  70.4 us

profile of v7, /device:TPU:0, one launch (start us, length us, event | category | flops | bytes accessed | tf_op | source)
XLA Modules:
  0.0 71.8 jit_solution(9472265764510933248)
XLA Ops:
  0.7 70.4 %shard_map.55 = bf16[8,8,3584]{2,1,0:T(8,128)(2,1)S(1)} custom-call(s32[1]{0:T(128)S(6)} %copy.7.offset_ref, s32[8,64]{1,0:T(8,128)} %bitcast.4, f32[8,64]{1,0:T(8,128)} %bitcast.5, bf16[64,8,2048]{2,1,0:T(8,128)(2,1)} %x_hbm.1, bf16[1,1024,3584]{2,1,0:T(8,128)(2,1)} %w_hbm.1), custom_call_target="tpu_custom_call" | custom-call | tf_op jit(solution)/shard_map/pallas_call | solution.py:497
  71.0 0.8 %copy.8 = bf16[64,3584]{1,0:T(8,128)(2,1)} copy(bf16[64,3584]{1,0:T(8,128)(2,1)S(1)} %bitcast.3) | data formatting | bytes 917504
